TPU v7x, 256 devices: a whole 4x4x8 slice. The times are simulated.
256 devices in a mesh: store: 16 (over z_lo, y), seq: 16 (over z_hi, x, core).
Axes of the slice: x: 4, y: 4, z: 8 (z_hi: 2, z_lo: 4; z = z_hi * 4 + z_lo), core: 2. Of those that a mesh axis runs over, the one named last changes fastest.
Arguments:
- store_kv: bfloat16 [256, 640, 2048], P('store', 'seq'), may hold values from -8 to 8
- span_len: int32 [16, 144], replicated, may hold values from 18 to 40, as said below
- span_shard: int32 [16, 16], replicated, may hold values from 0 to 15, each once within a row
- q_sel: bfloat16 [16, 1024, 8192], P('store', 'seq'), may hold values from -8 to 8
- fresh_kv: bfloat16 [16, 1024, 2048], P('store', 'seq'), may hold values from -8 to 8
- sel_pos: int32 [16, 1024], P('store', 'seq'), may hold values from -1 to 4095, as said below
Outputs:
- blended_kv: bfloat16 [16, 4096, 2048], P('store', 'seq')
- attn_out: bfloat16 [16, 1024, 8192], P('store', 'seq')
Inputs may be any that keep to these rules, and one draw needn't show every extreme that they name: `span_len`: each row sums to 4096, and its largest entry is 40. `span_shard`: each row names every store shard once. `sel_pos`: on seq index q, the 64 slots of a request hold distinct positions from q * 256 to (q + 1) * 256 - 1 in rising order, then -1 in unused slots; at least 2 slots are used, and in every draw some device uses all 64.
All inputs are finite; a program needn't handle non-finite values.
Results may differ from a plain program's by a relative error of at most 0.007.
Values may be sent and summed in bfloat16 or wider, within the bound.
No kernel may reach another device: no remote copies, remote signals or barrier semaphores. Data moves between devices by JAX's collectives and lax.ppermute only.
A program may use at most 192 MiB of HBM per device.

v0:
```python
import math

import jax
import jax.numpy as jnp
from jax import lax
from jax.sharding import PartitionSpec as P

HEADS = 64
KV_HEADS = 8
D_HEAD = 128
TOK_DEV = 256


ROPE_BASE = 500000.0


def rotate_keys(kv_rows, span_start):
    half_dim = D_HEAD // 2
    kv_width = KV_HEADS * D_HEAD
    row_count = kv_rows.shape[0]
    inverse = jnp.power(ROPE_BASE, -(jnp.arange(half_dim, dtype=jnp.float32) * 2.0 / D_HEAD))
    angles = span_start.astype(jnp.float32)[:, None] * inverse[None, :]
    cosine = jnp.cos(angles)[:, None, :]
    sine_part = jnp.sin(angles)[:, None, :]
    key_rows = kv_rows[:, :kv_width].reshape(row_count, KV_HEADS, D_HEAD)
    lower_half = key_rows[..., :half_dim]
    upper_half = key_rows[..., half_dim:]
    turned = jnp.concatenate(
        [
            lower_half * cosine - upper_half * sine_part,
            upper_half * cosine + lower_half * sine_part,
        ],
        axis=2,
    )
    return jnp.concatenate([turned.reshape(row_count, kv_width), kv_rows[:, kv_width:]], axis=1)


def locate(span_lengths, span_holders, positions):
    span_starts = jnp.cumsum(span_lengths) - span_lengths
    span_ids = jnp.arange(span_lengths.shape[0], dtype=jnp.int32)
    inside = (positions[:, None] >= span_starts[None, :]).astype(jnp.int32)
    which_span = jnp.sum(inside, axis=1) - 1
    picked = (which_span[:, None] == span_ids[None, :]).astype(jnp.int32)
    holder = jnp.sum(picked * span_holders[None, :], axis=1)
    span_start = jnp.sum(picked * span_starts[None, :], axis=1)
    return (holder, span_start)


def empty_states(row_count):
    groups = HEADS // KV_HEADS
    return (
        jnp.full((KV_HEADS, groups, row_count), -1e30, jnp.float32),
        jnp.zeros((KV_HEADS, groups, row_count), jnp.float32),
        jnp.zeros((KV_HEADS, groups, row_count, D_HEAD), jnp.float32),
    )


def absorb(states, queries, limits, kv_piece, first_row):

    def update(current):
        running_max, running_sum, weighted = current
        row_count = kv_piece.shape[0]
        kv_width = KV_HEADS * D_HEAD
        key_rows = kv_piece[:, :kv_width].reshape(row_count, KV_HEADS, D_HEAD)
        value_rows = kv_piece[:, kv_width:].reshape(row_count, KV_HEADS, D_HEAD)
        grouped = queries.reshape(queries.shape[0], KV_HEADS, HEADS // KV_HEADS, D_HEAD)
        scores = jnp.einsum(
            "qhgd,khd->hgqk", grouped, key_rows, preferred_element_type=jnp.float32
        ) / math.sqrt(D_HEAD)
        key_positions = jnp.arange(row_count, dtype=jnp.int32)
        allowed = (key_positions[None, :] <= limits[:, None])[None, None]
        piece_max = jnp.max(jnp.where(allowed, scores, -jnp.inf), axis=3)
        raised = jnp.maximum(running_max, piece_max)
        weights = jnp.where(allowed, jnp.exp(scores - raised[..., None]), 0.0)
        running_sum = jnp.sum(weights, axis=3)
        weighted = jnp.einsum(
            "hgqk,khd->hgqd",
            weights.astype(jnp.bfloat16),
            value_rows,
            preferred_element_type=jnp.float32,
        )
        return (raised, running_sum, weighted)

    useful = (first_row >= 0) & (first_row <= jnp.max(limits))
    return lax.cond(useful, update, lambda current: current, states)


def finish(states):
    running_max, running_sum, weighted = states
    normed = weighted / running_sum[..., None]
    return jnp.transpose(normed, (2, 0, 1, 3)).reshape(normed.shape[2], HEADS * D_HEAD)


def on_device(store_kv, span_len, span_shard, q_sel, fresh_kv, sel_pos):
    slot_rows = store_kv.shape[1]
    request = lax.axis_index("store")
    stripe = lax.axis_index("seq")
    fetched = lax.all_to_all(store_kv, "store", split_axis=0, concat_axis=0, tiled=True)
    lengths_row = lax.dynamic_index_in_dim(span_len, request, 0, keepdims=False)
    shards_row = lax.dynamic_index_in_dim(span_shard, request, 0, keepdims=False)
    holders_row = jnp.tile(shards_row, span_len.shape[1] // span_shard.shape[1])
    positions = stripe * TOK_DEV + jnp.arange(TOK_DEV, dtype=jnp.int32)
    holder, span_start = locate(lengths_row, holders_row, positions)
    offset = positions - jnp.maximum(span_start, stripe * TOK_DEV)
    flat_rows = fetched.reshape(-1, fetched.shape[2])
    cached = jnp.take(flat_rows, holder * slot_rows + offset, axis=0)
    rotated = rotate_keys(cached.astype(jnp.float32), span_start)
    chosen = sel_pos[0]
    matches = positions[:, None] == chosen[None, :]
    fresh_rows = jnp.dot(
        matches.astype(jnp.bfloat16), fresh_kv[0], preferred_element_type=jnp.float32
    )
    blended = jnp.where(jnp.any(matches, axis=1)[:, None], fresh_rows, rotated).astype(jnp.bfloat16)
    queries = q_sel[0]
    limits = jnp.maximum(chosen, 0)
    groups = ((queries, limits),)
    initial = tuple((empty_states(member[0].shape[0]) for member in groups))
    kv_piece = lax.all_gather(blended, "seq", axis=0, tiled=True)
    first_row = jnp.int32(0)
    finished = tuple(
        (
            absorb(member_state, member[0], member[1], kv_piece, first_row)
            for member_state, member in zip(initial, groups)
        )
    )
    attention = finish(finished[0]).astype(jnp.bfloat16)
    attended = jnp.where((chosen >= 0)[:, None], attention, jnp.zeros_like(attention))
    return (blended[None], attended[None])


def solution(mesh):
    return jax.shard_map(
        on_device,
        mesh=mesh,
        in_specs=(
            P("store", "seq", None),
            P(),
            P(),
            P("store", "seq", None),
            P("store", "seq", None),
            P("store", "seq"),
        ),
        out_specs=(P("store", "seq", None), P("store", "seq", None)),
        check_vma=False,
    )
```

profile of v0, /device:TPU:1, one launch (start us, length us, event | category | flops | bytes accessed | tf_op | source)
XLA Modules:
  0.0 371.7 jit_solution(6813124720219924720)
XLA Ops:
  7.2 0.0 copy-start
  7.2 0.0 copy-start.3
  7.2 9.3 %all-to-all-start = ((bf16[16,40,2048]{2,1,0:T(8,128)(2,1)}), bf16[16,40,2048]{2,1,0:T(8,128)(2,1)S(1)}, u32[]{:S(2)}, u32[]{:S(2)}) async-start(bf16[16,40,2048]{2,1,0:T(8,128)(2,1)} %param.8), calls=%async_computation | async-start | bytes 5242880 | tf_op jit(solution)/shard_map/all_to_all | solution.py:98
  16.5 0.0 all-gather.2.cloned.1.call-start
  16.6 0.7 constant_dynamic-slice_fusion
  17.3 0.3 reduce-window.9
  17.6 0.1 slice.28
  17.7 0.7 dynamic-slice_bitcast_fusion
  18.4 0.1 mul.90
  18.5 0.1 slice_reduce_fusion
  18.6 0.1 add_bitcast_fusion
  18.7 0.1 convert_reduce_fusion
  18.8 0.1 select_reduce_fusion
  19.0 0.7 compare_reduce_fusion
  19.8 0.5 multiply_cosine_fusion
  20.3 46.9 %all-to-all-done = bf16[16,40,2048]{2,1,0:T(8,128)(2,1)S(1)} async-done(((bf16[16,40,2048]{2,1,0:T(8,128)(2,1)}), bf16[16,40,2048]{2,1,0:T(8,128)(2,1)S(1)}, u32[]{:S(2)}, u32[]{:S(2)}) %all-to-all-start) | async-done | bytes 2621472 | tf_op jit(solution)/shard_map/all_to_all | solution.py:98
  67.2 2.3 gather_fusion
  69.5 1.4 select_convert_fusion
  70.9 0.1 slice_bitcast_fusion
  71.0 0.1 slice.42
  71.1 0.2 copy.28
  71.3 0.5 multiply_subtract_fusion
  71.8 0.3 pad_maximum_fusion
  72.1 0.1 copy.35
  72.2 0.0 copy-done
  72.2 0.0 copy-done.3
  72.3 1.5 fusion.12
  73.8 0.0 all-gather.2.cloned.1.call-update
  73.8 0.6 broadcast_maximum_fusion.2
  75.1 182.5 %all-gather.2.cloned.1.call-done = bf16[4096,2048]{1,0:T(8,128)(2,1)} async-done(((bf16[256,2048]{1,0:T(8,128)(2,1)}), bf16[4096,2048]{1,0:T(8,128)(2,1)}) %all-gather.2.cloned.1.call-update) | async-done | bytes 16777232 | tf_op jit(solution)/shard_map/all_gather | solution.py:118
  257.6 103.0 %conditional.1 = (f32[8,8,64]{2,1,0:T(8,128)S(1)}, f32[8,8,64,128]{3,2,1,0:T(8,128)}) conditional(s32[]{:T(128)} %convert_element_type.44, () %tuple.16, (s32[64]{0:T(128)S(1)}, bf16[4096,2048]{1,0:T(8,128)(2,1)}, bf16[1,64,8192]{2,1,0:T(8,128)(2,1)}) %tuple.17), branch_computations={%region_7.8_spmd, %region_8.11_spmd} | conditional | flops 8774742016 | bytes 295797056 | solution.py:85
  257.6 0.2 iota_compare_fusion
  257.8 20.7 %copy.19 = bf16[4096,2048]{0,1:T(8,128)(2,1)} copy(bf16[4096,2048]{1,0:T(8,128)(2,1)} %get-tuple-element.21) | data formatting | bytes 33554432 | tf_op jit(solution)/shard_map
  278.5 0.0 copy-start.2
  278.5 9.5 %fusion.19 = (bf16[4096,1024]{0,1:T(8,128)(2,1)}, bf16[4096,1024]{0,1:T(8,128)(2,1)S(1)}) fusion(bf16[4096,2048]{0,1:T(8,128)(2,1)} %copy.19), kind=kLoop, calls=%fused_computation.56 | loop fusion | bytes 33554432 | tf_op jit(solution)/shard_map/cond/branch_1_fun/slice | solution.py:65
  288.0 0.0 copy-done.2
  288.0 0.3 copy.27
  288.3 23.6 %fusion = (f32[8,8,64]{2,1,0:T(8,128)S(1)}, f32[8,4096,64,8]{1,2,3,0:T(8,128)}) fusion(pred[64,4096]{1,0:T(8,128)(4,1)S(1)} %iota_compare_fusion, bf16[4096,8,128,1]{0,2,3,1:T(8,128)(2,1)S(1)} %bitcast.62, bf16[64,8,8,128]{3,2,1,0:T(8,128)(2,1)S(1)} %bitcast.65), kind=kOutput, calls=%fused_computation.3 | convolution fusion | flops 4345294848 | bytes 76824576 | tf_op jit(solution)/shard_map/cond/branch_1_fun/qhgd,khd->hgqk/dot_general | solution.py:67
  311.9 27.0 %fusion.5 = f32[8,8,64,128]{3,2,1,0:T(8,128)} fusion(bf16[4096,8,128,1]{0,2,3,1:T(8,128)(2,1)} %bitcast.64, f32[8,4096,64,8]{1,2,3,0:T(8,128)} %get-tuple-element.30, f32[8,8,64]{2,1,0:T(8,128)S(1)} %broadcast_maximum_fusion, pred[64,4096]{1,0:T(8,128)(4,1)S(1)} %iota_compare_fusion), kind=kOutput, calls=%fused_computation.8 | convolution fusion | flops 4362076160 | bytes 77873152 | tf_op jit(solution)/shard_map/cond/branch_1_fun/hgqk,khd->hgqd/dot_general | solution.py:76
  338.9 21.6 %fusion.4 = f32[8,8,64]{2,1,0:T(8,128)S(1)} fusion(f32[8,4096,64,8]{1,2,3,0:T(8,128)} %get-tuple-element.30, f32[8,8,64]{2,1,0:T(8,128)S(1)} %broadcast_maximum_fusion, pred[64,4096]{1,0:T(8,128)(4,1)S(1)} %iota_compare_fusion), kind=kLoop, calls=%fused_computation.7 | loop fusion | flops 67104768 | bytes 67403776 | tf_op jit(solution)/shard_map/cond/branch_1_fun/reduce_sum | solution.py:75
  360.6 0.0 copy-start.1
  360.6 2.0 fusion.13
  362.6 0.7 copy.20
  363.3 0.5 convert_element_type.47
  363.8 1.1 broadcast_select_fusion
  364.9 0.0 copy-done.1
  (14 shorter events, 0.1 us)
Async XLA Ops:
  7.2 65.1 %copy-start = (bf16[1,64,2048]{2,1,0:T(8,128)(2,1)S(1)}, bf16[1,64,2048]{2,1,0:T(8,128)(2,1)}, u32[]{:S(2)}) copy-start(bf16[1,64,2048]{2,1,0:T(8,128)(2,1)} %param.12) | copy-start | bytes 786436
  7.2 65.1 %copy-start.3 = (s32[1,64]{1,0:T(1,128)S(1)}, s32[1,64]{1,0:T(1,128)}, u32[]{:S(2)}) copy-start(s32[1,64]{1,0:T(1,128)} %param.13) | copy-start | bytes 772
  7.2 60.0 %all-to-all-start = ((bf16[16,40,2048]{2,1,0:T(8,128)(2,1)}), bf16[16,40,2048]{2,1,0:T(8,128)(2,1)S(1)}, u32[]{:S(2)}, u32[]{:S(2)}) async-start(bf16[16,40,2048]{2,1,0:T(8,128)(2,1)} %param.8), calls=%async_computation | async-start | bytes 5242880 | tf_op jit(solution)/shard_map/all_to_all | solution.py:98
  16.5 241.0 %all-gather.2.cloned.1.call-start = ((), (), s32[]{:S(2)}) async-start(), calls=%async_computation.1 | async-start | bytes 17825792 | tf_op jit(solution)/shard_map/all_gather | solution.py:118
  278.5 9.5 %copy-start.2 = (bf16[1,64,8192]{2,1,0:T(8,128)(2,1)S(1)}, bf16[1,64,8192]{2,1,0:T(8,128)(2,1)}, u32[]{:S(2)}) copy-start(bf16[1,64,8192]{2,1,0:T(8,128)(2,1)} %get-tuple-element.16) | copy-start | bytes 3145732 | tf_op jit(solution)/shard_map/cond
  360.6 4.3 %copy-start.1 = (bf16[1,64,2048]{2,1,0:T(8,128)(2,1)S(1)}, bf16[1,64,2048]{2,1,0:T(8,128)(2,1)}, u32[]{:S(2)}) copy-start(bf16[1,64,2048]{2,1,0:T(8,128)(2,1)} %param.12) | copy-start | bytes 786436
Sparse Core Ops, SparseCore 0:
  73.9 183.5 all-gather.1
where the time goes:
time: 373 us; the launch traced here: 372 us
  waiting for transfers between devices  229 us (61%)
  matrix products  52.2 us (14%)
  local copies, waits for them, and re-layouts  36.2 us (10%)
  other arithmetic  29.8 us (8%)
  between operations  14.9 us (4%)
  starting transfers between devices  9.36 us (3%)
    all_gather x1, waiting for transfers between devices, on_device(): kv_piece = lax.all_gather(blended, 'seq', axis=0, tiled=True)  182 us
    all_to_all x1, waiting for transfers between devices, on_device(): lax.all_to_all(store_kv, 'store', split_axis=0, concat_axis=0, tiled=True)  46.9 us
    dot_general x1, matrix products, update(): jnp.einsum('hgqk,khd->hgqd', weights.astype(jnp.bfloat16), value_rows, pr...  27 us
    dot_general x1, matrix products, update(): jnp.einsum('qhgd,khd->hgqk', grouped, key_rows, preferred_element_type=jn...  23.6 us
    reduce_sum x1, other arithmetic, update(): running_sum = jnp.sum(weights, axis=3)  21.6 us
    another operation x2, local copies, waits for them, and re-layouts  20.9 us
    slice x1, local copies, waits for them, and re-layouts, update(): value_rows = kv_piece[:, kv_width:].reshape(row_count, KV_HEADS, D_HEAD)  9.49 us
    all_to_all x1, starting transfers between devices, on_device(): lax.all_to_all(store_kv, 'store', split_axis=0, concat_axis=0, tiled=True)  9.32 us
  transfers between devices with their start and end apart: 2, of which 2 were waited for; matrix products, arithmetic and copies ran while one was open for 1% of the time, Pallas kernels for 0%

commit v1 on v0

v1 whole, which is shorter than its diff:
```python
import functools
import math

import jax
import jax.numpy as jnp
from jax import lax
from jax.experimental import pallas as pl
from jax.experimental.pallas import tpu as pltpu
from jax.sharding import PartitionSpec as P

HEADS = 64
KV_HEADS = 8
D_HEAD = 128
TOK_DEV = 256
SEL_DEV = 64
GROUPS = HEADS // KV_HEADS
KV_WIDTH = KV_HEADS * D_HEAD
Q_WIDTH = GROUPS * D_HEAD
ROWS = GROUPS * SEL_DEV
HALF = 8
ROPE_BASE = 500000.0
EXP_SCALE = math.log2(math.e) / math.sqrt(D_HEAD)
VMEM_LIMIT = 32 * 1024 * 1024


VMEM = pl.BlockSpec(memory_space=pltpu.VMEM)
SMEM = pl.BlockSpec(memory_space=pltpu.SMEM)


def params(**more):
    return pltpu.CompilerParams(vmem_limit_bytes=VMEM_LIMIT, **more)


def locate(span_lengths, span_holders, positions):
    span_starts = jnp.cumsum(span_lengths) - span_lengths
    span_ids = jnp.arange(span_lengths.shape[0], dtype=jnp.int32)
    inside = (positions[:, None] >= span_starts[None, :]).astype(jnp.int32)
    which_span = jnp.sum(inside, axis=1) - 1
    picked = (which_span[:, None] == span_ids[None, :]).astype(jnp.int32)
    holder = jnp.sum(picked * span_holders[None, :], axis=1)
    span_start = jnp.sum(picked * span_starts[None, :], axis=1)
    return (holder, span_start)


def spread_kernel(me_ref, q_ref, loc_ref, *out_refs):
    me = me_ref[0]
    for shift, out_ref in enumerate(out_refs):
        head = lax.rem(me + shift, HALF)
        columns = pl.ds(pl.multiple_of(head * Q_WIDTH, Q_WIDTH), Q_WIDTH)
        out_ref[:, :Q_WIDTH] = q_ref[:, columns]
        out_ref[:, Q_WIDTH:] = loc_ref[...]


def spread_queries(me, queries, local):
    shape = jax.ShapeDtypeStruct((SEL_DEV, Q_WIDTH + D_HEAD), jnp.bfloat16)
    return pl.pallas_call(
        spread_kernel,
        out_shape=(shape,) * HALF,
        in_specs=[SMEM, VMEM, VMEM],
        out_specs=(VMEM,) * HALF,
        compiler_params=params(),
        name="spread_queries",
    )(me, queries, local)


def blend_kernel(me_ref, pick_ref, match_ref, cos_ref, sin_ref, rows_ref, fresh_ref, blended_ref, *out_refs):
    me = me_ref[0]
    half_dim = D_HEAD // 2
    for shift, out_ref in enumerate(out_refs):
        head = lax.rem(me + shift, HALF)
        key_columns = pl.ds(pl.multiple_of(head * D_HEAD, D_HEAD), D_HEAD)
        value_columns = pl.ds(pl.multiple_of(KV_WIDTH + head * D_HEAD, D_HEAD), D_HEAD)
        both = jnp.concatenate([rows_ref[:, key_columns], rows_ref[:, value_columns]], axis=1)
        both_fresh = jnp.concatenate([fresh_ref[:, key_columns], fresh_ref[:, value_columns]], axis=1)
        rows = jnp.dot(pick_ref[...], both, preferred_element_type=jnp.float32)
        rows += jnp.dot(match_ref[...], both_fresh, preferred_element_type=jnp.float32)
        keys = rows[:, :D_HEAD]
        keys = keys * cos_ref[...] + pltpu.roll(keys, half_dim, 1) * sin_ref[...]
        rows = jnp.concatenate([keys, rows[:, D_HEAD:]], axis=1).astype(jnp.bfloat16)
        blended_ref[:, key_columns] = rows[:, :D_HEAD]
        blended_ref[:, value_columns] = rows[:, D_HEAD:]
        out_ref[...] = rows


def blend(me, pick, match, cosine, sine, rows, fresh):
    piece = jax.ShapeDtypeStruct((TOK_DEV, 2 * D_HEAD), jnp.bfloat16)
    whole = jax.ShapeDtypeStruct((TOK_DEV, 2 * KV_WIDTH), jnp.bfloat16)
    return pl.pallas_call(
        blend_kernel,
        out_shape=(whole,) + (piece,) * HALF,
        in_specs=[SMEM] + [VMEM] * 6,
        out_specs=(VMEM,) * (HALF + 1),
        compiler_params=params(),
        cost_estimate=pl.CostEstimate(flops=2 * TOK_DEV * 704 * 2 * KV_WIDTH, bytes_accessed=6_000_000, transcendentals=0),
        name="blend",
    )(me, pick, match, cosine, sine, rows, fresh)


BLOCK = 256


def scores_of(q_ref, slot, block, keys):
    heads = range(block * BLOCK // SEL_DEV, (block + 1) * BLOCK // SEL_DEV)
    rows = jnp.concatenate([q_ref[slot, :, g * D_HEAD:(g + 1) * D_HEAD] for g in heads], axis=0)
    return lax.dot_general(rows, keys, (((1,), (1,)), ((), ())), preferred_element_type=jnp.float32)


def widen(column):
    return jnp.broadcast_to(column, (BLOCK, D_HEAD))


def weigh(scores, values, top, total, weighted):
    tiles = scores.shape[1] // D_HEAD
    raised = widen(jnp.max(scores, axis=1, keepdims=True))
    if top is not None:
        raised = jnp.maximum(top, raised)
    weights = jnp.exp2((scores - jnp.concatenate([raised] * tiles, axis=1)) * EXP_SCALE)
    partial = weights[:, :D_HEAD]
    for tile in range(1, tiles):
        partial += weights[:, tile * D_HEAD:(tile + 1) * D_HEAD]
    product = jnp.dot(weights.astype(jnp.bfloat16), values, preferred_element_type=jnp.float32)
    if top is not None:
        shrink = jnp.exp2((top - raised) * EXP_SCALE)
        partial += total * shrink
        product += weighted * shrink
    return raised, partial, product


def local_kernel(me_ref, q_ref, *refs):
    kv_refs, (top_ref, total_ref, acc_ref, held) = refs[:HALF], refs[HALF:]
    me = me_ref[0]
    for shift, kv_ref in enumerate(kv_refs):
        held[pl.ds(pl.multiple_of(lax.rem(me - shift + HALF, HALF) * TOK_DEV, TOK_DEV), TOK_DEV)] = kv_ref[...]

    def attend(slot, stripe, size):
        local = q_ref[slot, :, Q_WIDTH:Q_WIDTH + 1].astype(jnp.float32)
        local += (stripe * TOK_DEV - (size - 2 * TOK_DEV)).astype(jnp.float32)
        key = lax.broadcasted_iota(jnp.int32, (SEL_DEV, 2 * TOK_DEV), 1).astype(jnp.float32)
        penalty = jnp.where(key <= local, 0.0, -1e30)
        penalty = jnp.concatenate([penalty] * (BLOCK // SEL_DEV), axis=0)
        keys, values = held[:size, :D_HEAD], held[:size, D_HEAD:]
        scored = [scores_of(q_ref, slot, block, keys) for block in range(ROWS // BLOCK)]
        for block, scores in enumerate(scored):
            tail = scores[:, size - 2 * TOK_DEV:] + penalty
            scores = tail if size == 2 * TOK_DEV else jnp.concatenate([scores[:, :size - 2 * TOK_DEV], tail], axis=1)
            rows = pl.ds(block * BLOCK, BLOCK)
            top_ref[slot, rows], total_ref[slot, rows], acc_ref[slot, rows] = weigh(scores, values, None, None, None)

    def step(slot, carry):
        stripe = lax.rem(me - slot + HALF, HALF)
        for pair in range(HALF // 2):
            @pl.when(stripe // 2 == pair)
            def _(pair=pair):
                attend(slot, stripe, (pair + 1) * 2 * TOK_DEV)
        return carry

    lax.fori_loop(0, HALF, step, 0)


STATE = jax.ShapeDtypeStruct((HALF, ROWS, D_HEAD), jnp.float32)
UNIT_FLOPS = 4 * ROWS * TOK_DEV * D_HEAD


def attend_local(me, queries, pieces):
    return pl.pallas_call(
        local_kernel,
        out_shape=(STATE,) * 3,
        in_specs=[SMEM, VMEM] + [VMEM] * HALF,
        out_specs=(VMEM,) * 3,
        scratch_shapes=[pltpu.VMEM((HALF * TOK_DEV, 2 * D_HEAD), jnp.bfloat16)],
        compiler_params=params(),
        cost_estimate=pl.CostEstimate(flops=36 * UNIT_FLOPS, bytes_accessed=6_000_000, transcendentals=36 * ROWS * TOK_DEV),
        name="attend_local",
    )(me, queries, *pieces)


def cross_kernel(count, slots, upper_ref, q_ref, *refs):
    kv_refs, state_refs, out_refs = refs[:count], refs[count:count + 3], refs[count + 3:]
    last = slots is not None
    if last:
        out_refs, normed_ref = out_refs[:-1], out_refs[-1]

    def put(index, slot, block, top, total, weighted):
        if not last:
            for out_ref, value in zip(out_refs, (top, total, weighted)):
                out_ref[slot, pl.ds(block * BLOCK, BLOCK)] = value
            return
        normed = (weighted / jnp.sum(total, axis=1, keepdims=True)).astype(jnp.bfloat16)
        for g in range(BLOCK // SEL_DEV):
            first = (block * BLOCK // SEL_DEV + g) * D_HEAD
            normed_ref[index, :, first:first + D_HEAD] = normed[g * SEL_DEV:(g + 1) * SEL_DEV]

    def states(slot, block):
        return [ref[slot, pl.ds(block * BLOCK, BLOCK)] for ref in state_refs]

    def attend(index, slot):
        kv = jnp.concatenate([kv_ref[...] for kv_ref in kv_refs], axis=0)
        scored = [scores_of(q_ref, slot, block, kv[:, :D_HEAD]) for block in range(ROWS // BLOCK)]
        for block, scores in enumerate(scored):
            put(index, slot, block, *weigh(scores, kv[:, D_HEAD:], *states(slot, block)))

    def keep(index, slot):
        for block in range(ROWS // BLOCK):
            put(index, slot, block, *states(slot, block))

    def each(visit):
        def step(index, carry):
            slot = index
            if last:
                slot = jnp.int32(slots[0])
                for at, value in enumerate(slots):
                    slot = jnp.where(index == at, value, slot)
            visit(index, slot)
            return carry

        lax.fori_loop(0, len(slots) if last else HALF, step, 0)

    @pl.when(upper_ref[0] == 1)
    def _():
        each(attend)

    if last:
        @pl.when(upper_ref[0] == 0)
        def _():
            each(keep)

        for index, out_ref in enumerate(out_refs):
            out_ref[...] = normed_ref[index]


def attend_cross(upper, queries, pieces, state, slots=None):
    count = len(pieces)
    if slots is None:
        part, scratch = HALF, []
        out_shape, aliases = (STATE,) * 3, {2 + count + i: i for i in range(3)}
    else:
        part = len(slots)
        scratch = [pltpu.VMEM((part, SEL_DEV, Q_WIDTH), jnp.bfloat16)]
        out_shape, aliases = (jax.ShapeDtypeStruct((SEL_DEV, Q_WIDTH), jnp.bfloat16),) * part, {}
    return pl.pallas_call(
        functools.partial(cross_kernel, count, slots),
        out_shape=out_shape,
        in_specs=[SMEM, VMEM] + [VMEM] * (count + 3),
        out_specs=(VMEM,) * len(out_shape),
        scratch_shapes=scratch,
        input_output_aliases=aliases,
        compiler_params=params(),
        cost_estimate=pl.CostEstimate(flops=part * count * UNIT_FLOPS, bytes_accessed=6_000_000, transcendentals=part * count * ROWS * TOK_DEV),
        name="attend_cross",
    )(upper, queries, *pieces, *state)


def place_kernel(me_ref, used_ref, *refs):
    pieces, out_ref = refs[:HALF], refs[HALF]
    me = me_ref[0]
    used = used_ref[...] > 0
    for shift, piece in enumerate(pieces):
        head = lax.rem(me + shift, HALF)
        columns = pl.ds(pl.multiple_of(head * Q_WIDTH, Q_WIDTH), Q_WIDTH)
        out_ref[:, columns] = jnp.where(used, piece[...], jnp.zeros_like(piece))


def place_heads(me, used, pieces):
    return pl.pallas_call(
        place_kernel,
        out_shape=jax.ShapeDtypeStruct((SEL_DEV, HEADS * D_HEAD), jnp.bfloat16),
        in_specs=[SMEM, VMEM] + [VMEM] * HALF,
        out_specs=VMEM,
        compiler_params=params(),
        name="place_heads",
    )(me, used, *pieces)


CLIMBS = (0, 1, 7, 2, 6, 3, 5, 4)
FIRST_SLOTS, LAST_SLOTS = (4, 3, 5, 2), (6, 1, 7, 0)


def on_device(store_kv, span_len, span_shard, q_sel, fresh_kv, sel_pos):
    slot_rows = store_kv.shape[1]
    request = lax.axis_index("store")
    stripe = lax.axis_index("seq")
    upper = (stripe // HALF).astype(jnp.int32)[None]
    me = lax.rem(stripe, HALF).astype(jnp.int32)[None]

    def turn(value, shift):
        pairs = [(h * HALF + i, h * HALF + (i + shift) % HALF) for h in range(2) for i in range(HALF)]
        return lax.ppermute(value, "seq", pairs)

    def climb(value):
        return lax.ppermute(value, "seq", [(i, HALF + i) for i in range(HALF)])

    fetched = lax.all_to_all(store_kv, "store", split_axis=0, concat_axis=0, tiled=True)

    chosen = sel_pos[0]
    base = stripe * TOK_DEV
    local = jnp.maximum(chosen - base, 0).astype(jnp.bfloat16)
    spread = spread_queries(me, q_sel[0], jnp.broadcast_to(local[:, None], (SEL_DEV, D_HEAD)))
    arrived = [spread[0]] + [turn(spread[s], s) for s in range(1, HALF)]
    queries = jnp.stack(arrived)

    lengths_row = lax.dynamic_index_in_dim(span_len, request, 0, keepdims=False)
    shards_row = lax.dynamic_index_in_dim(span_shard, request, 0, keepdims=False)
    holders_row = jnp.tile(shards_row, span_len.shape[1] // span_shard.shape[1])
    positions = base + jnp.arange(TOK_DEV, dtype=jnp.int32)
    holder, span_start = locate(lengths_row, holders_row, positions)
    row = holder * slot_rows + positions - jnp.maximum(span_start, base)
    matches = positions[:, None] == chosen[None, :]
    renewed = jnp.any(matches, axis=1)[:, None]
    row_ids = jnp.arange(store_kv.shape[0] * slot_rows, dtype=jnp.int32)
    pick = ((row[:, None] == row_ids[None, :]) & ~renewed).astype(jnp.bfloat16)
    half_dim = D_HEAD // 2
    inverse = jnp.power(ROPE_BASE, -(jnp.arange(half_dim, dtype=jnp.float32) * 2.0 / D_HEAD))
    angles = span_start.astype(jnp.float32)[:, None] * inverse[None, :]
    cosine = jnp.where(renewed, 1.0, jnp.cos(angles))
    sine = jnp.where(renewed, 0.0, jnp.sin(angles))
    cosine = jnp.concatenate([cosine, cosine], axis=1)
    sine = jnp.concatenate([-sine, sine], axis=1)

    fetched, queries = lax.optimization_barrier((fetched, queries))
    blended, *own = blend(
        me, pick, matches.astype(jnp.bfloat16), cosine, sine, fetched.reshape(-1, fetched.shape[2]), fresh_kv[0]
    )
    near, far = [own[0]], []
    for s in range(1, HALF):
        near.append(turn(own[s], s))
    for s in range(HALF):
        far.append(climb(near[s]))

    state = attend_local(me, queries, near)
    state = attend_cross(upper, queries, [far[s] for s in CLIMBS[:4]], state)
    results = {}
    for slots in (FIRST_SLOTS, LAST_SLOTS):
        results |= dict(zip(slots, attend_cross(upper, queries, [far[s] for s in CLIMBS[4:]], state, slots)))

    heads = [results[0]]
    for s in range(1, HALF):
        heads.append(turn(results[s], HALF - s))
    used = jnp.broadcast_to((chosen >= 0).astype(jnp.int32)[:, None], (SEL_DEV, 1))
    attended = place_heads(me, used, heads)
    return (blended[None], attended[None])


def solution(mesh):
    return jax.shard_map(
        on_device,
        mesh=mesh,
        in_specs=(
            P("store", "seq", None),
            P(),
            P(),
            P("store", "seq", None),
            P("store", "seq", None),
            P("store", "seq"),
        ),
        out_specs=(P("store", "seq", None), P("store", "seq", None)),
        check_vma=False,
    )
```

time: 373 us -> 168 us (0.45)
  the two profiles are of different devices: /device:TPU:1 before, /device:TPU:176 now
where the time goes in v1:
time: 168 us
  waiting for transfers between devices  86.9 us (52%)
  starting transfers between devices  42 us (25%)
  Pallas kernels  30 us (18%)
  local copies, waits for them, and re-layouts  5.28 us (3%)
  other arithmetic  2.39 us (1%)
    all_to_all x1, waiting for transfers between devices, on_device(): lax.all_to_all(store_kv, 'store', split_axis=0, concat_axis=0, tiled=True)  50.2 us
    ppermute x8, waiting for transfers between devices, climb(): return lax.ppermute(value, 'seq', [(i, HALF + i) for i in range(HALF)])  26 us
    ppermute x21, starting transfers between devices, turn(): return lax.ppermute(value, 'seq', pairs)  25 us
    pallas_call x3, Pallas kernels, attend_cross(): pl.pallas_call(functools.partial(cross_kernel, count, slots), out_shape=o...  15.5 us
    ppermute x21, waiting for transfers between devices, turn(): return lax.ppermute(value, 'seq', pairs)  10.8 us
    ppermute x8, starting transfers between devices, climb(): return lax.ppermute(value, 'seq', [(i, HALF + i) for i in range(HALF)])  10.4 us
    pallas_call x1, Pallas kernels, attend_local(): pl.pallas_call(local_kernel, out_shape=(STATE,) * 3, in_specs=[SMEM, VMEM...  8.87 us
    all_to_all x1, starting transfers between devices, on_device(): lax.all_to_all(store_kv, 'store', split_axis=0, concat_axis=0, tiled=True)  6.63 us
  transfers between devices with their start and end apart: 30, of which 17 were waited for; matrix products, arithmetic and copies ran while one was open for 3% of the time, Pallas kernels for 12%

profile of v1, /device:TPU:176, one launch (start us, length us, event | category | flops | bytes accessed | tf_op | source)
XLA Modules:
  0.0 167.6 jit_solution(12015086194065179863)
XLA Ops:
  0.7 0.7 maximum_convert_fusion
  1.4 1.2 copy-done.1
  2.6 0.1 spread_queries.1
  2.7 1.6 collective-permute-start.1
  4.3 2.0 %collective-permute-start.2 = (bf16[64,1152]{1,0:T(8,128)(2,1)S(1)}, bf16[64,1152]{1,0:T(8,128)(2,1)}, u32[]{:S(2)}, u32[]{:S(2)}) collective-permute-start(bf16[64,1152]{1,0:T(8,128)(2,1)S(1)} %get-tuple-element.38), channel_id=1, source_target_pairs={{0,3},{1,4},{2,5},{3,6},{4,7},{5,0},{6,1},{7,2},{8,11},{9,12},{10,... | collective-permute-start | bytes 442376 | tf_op jit(solution)/shard_map/ppermute | solution.py:287
  6.3 2.0 %collective-permute-start.3 = (bf16[64,1152]{1,0:T(8,128)(2,1)S(1)}, bf16[64,1152]{1,0:T(8,128)(2,1)S(1)}, u32[]{:S(2)}, u32[]{:S(2)}) collective-permute-start(bf16[64,1152]{1,0:T(8,128)(2,1)S(1)} %get-tuple-element.39), channel_id=1, source_target_pairs={{0,4},{1,5},{2,6},{3,7},{4,0},{5,1},{6,2},{7,3},{8,12},{9,13},{10,... | collective-permute-start | bytes 442376 | tf_op jit(solution)/shard_map/ppermute | solution.py:287
  8.4 1.7 collective-permute-start.4
  10.0 6.6 %all-to-all-start = ((bf16[16,40,2048]{2,1,0:T(8,128)(2,1)}), bf16[16,40,2048]{2,1,0:T(8,128)(2,1)}, u32[]{:S(2)}, u32[]{:S(2)}) async-start(bf16[16,40,2048]{2,1,0:T(8,128)(2,1)} %param.6), calls=%async_computation | async-start | bytes 5242880 | tf_op jit(solution)/shard_map/all_to_all | solution.py:292
  16.7 0.3 reduce-window.9
  17.1 0.1 slice_reduce_fusion
  17.3 0.7 dynamic-slice_bitcast_fusion
  18.0 0.1 mul.46
  18.1 0.1 convert_reduce_fusion
  18.2 0.2 compare_convert_fusion
  18.4 0.1 select_reduce_fusion.1
  18.5 0.6 fusion.4
  19.1 0.2 fusion.1.pick_ref
  19.3 0.1 pad_maximum_fusion
  19.5 1.5 collective-permute-start.5
  21.0 0.9 bitcast_dynamic-update-slice_fusion.6
  22.0 0.9 bitcast_dynamic-update-slice_fusion.5
  22.9 0.9 bitcast_dynamic-update-slice_fusion.4
  23.9 0.8 collective-permute-done.5
  24.7 0.5 collective-permute-done.6
  25.2 50.2 %all-to-all-done = bf16[16,40,2048]{2,1,0:T(8,128)(2,1)} async-done(((bf16[16,40,2048]{2,1,0:T(8,128)(2,1)}), bf16[16,40,2048]{2,1,0:T(8,128)(2,1)}, u32[]{:S(2)}, u32[]{:S(2)}) %all-to-all-start) | async-done | bytes 2621472 | tf_op jit(solution)/shard_map/all_to_all | solution.py:292
  75.4 4.4 %blend.1 = (bf16[256,2048]{1,0:T(8,128)(2,1)}, bf16[256,256]{1,0:T(8,128)(2,1)S(1)}, bf16[256,256]{1,0:T(8,128)(2,1)S(1)}, bf16[256,256]{1,0:T(8,128)(2,1)S(1)},...) custom-call(s32[1]{0:T(128)} %bitcast.me_ref, ...), custom_call_target="tpu_custom_call" | custom-call | flops 738197504 | bytes 6000000 | tf_op jit(solution)/shard_map/blend/pallas_call | solution.py:88
  79.8 0.9 collective-permute-start.11
  80.7 1.4 collective-permute-start.13
  82.1 0.5 collective-permute-start.16
  82.6 2.4 %collective-permute-start.18 = (bf16[256,256]{1,0:T(8,128)(2,1)S(1)}, bf16[256,256]{1,0:T(8,128)(2,1)S(1)}, u32[]{:S(2)}, u32[]{:S(2)}) collective-permute-start(bf16[256,256]{1,0:T(8,128)(2,1)S(1)} %get-tuple-element.52), channel_id=1, source_target_pairs={{0,7},{1,0},{2,1},{3,2},{4,3},{5,4},{6,5},{7,6},{8,15},{9,8},{10,9... | collective-permute-start | bytes 393224 | tf_op jit(solution)/shard_map/ppermute | solution.py:287
  85.0 0.2 collective-permute-done.11.refs_5_
  85.2 3.0 %collective-permute-start.7 = (bf16[256,256]{1,0:T(8,128)(2,1)S(1)}, bf16[256,256]{1,0:T(8,128)(2,1)S(1)}, u32[]{:S(2)}, u32[]{:S(2)}) collective-permute-start(bf16[256,256]{1,0:T(8,128)(2,1)S(1)} %get-tuple-element.46), channel_id=1, source_target_pairs={{0,6},{1,7},{2,0},{3,1},{4,2},{5,3},{6,4},{7,5},{8,14},{9,15},{10,... | collective-permute-start | bytes 393224 | tf_op jit(solution)/shard_map/ppermute | solution.py:287
  88.3 0.3 collective-permute-done.13.refs_4_
  88.6 0.6 collective-permute-done.16.refs_1_
  89.2 1.3 collective-permute-start.15
  90.5 1.3 collective-permute-start.17
  91.8 0.2 collective-permute-done.20.refs_2_
  92.0 1.3 collective-permute-start.19
  93.3 1.3 collective-permute-start.21
  94.6 1.2 collective-permute-done.9.refs_3_
  95.8 1.5 collective-permute-start.10
  97.3 8.9 %attend_local.1 = (f32[8,512,128]{2,1,0:T(8,128)S(1)}, f32[8,512,128]{2,1,0:T(8,128)S(1)}, f32[8,512,128]{2,1,0:T(8,128)S(1)}) custom-call(s32[1]{0:T(128)} %bitcast.me_ref, bf16[8,64,1152]{2,1,0:T(8,128)(2,1)S(1)} %bitcast_dynamic-update-slice_fusion.q_ref, bf16[256,256]{1,0:T(8,128)(2,1)S(1)} %get-tuple-element.50.refs_0_, ...), custom_call_target="tpu_custom_call" | custom-call | flops 2415919104 | bytes 6000000 | tf_op jit(solution)/shard_map/attend_local/pallas_call | solution.py:165
  106.1 17.7 %collective-permute-done.15.refs_0_ = bf16[256,256]{1,0:T(8,128)(2,1)S(1)} collective-permute-done((bf16[256,256]{1,0:T(8,128)(2,1)S(1)}, bf16[256,256]{1,0:T(8,128)(2,1)S(1)}, u32[]{:S(2)}, u32[]{:S(2)}) %collective-permute-start.15) | collective-permute-done | bytes 131104 | tf_op jit(solution)/shard_map/ppermute | solution.py:290
  123.8 1.3 collective-permute-start.12
  125.1 1.5 collective-permute-done.17.refs_1_
  126.6 1.3 collective-permute-start.14
  127.9 1.5 collective-permute-done.19.refs_2_
  129.4 1.3 collective-permute-start.8
  130.7 1.5 collective-permute-done.21.refs_3_
  132.2 7.4 %attend_cross.3 = (f32[8,512,128]{2,1,0:T(8,128)S(1)}, f32[8,512,128]{2,1,0:T(8,128)S(1)}, f32[8,512,128]{2,1,0:T(8,128)S(1)}) custom-call(s32[1]{0:T(128)} %bitcast.19.upper_ref, bf16[8,64,1152]{2,1,0:T(8,128)(2,1)S(1)} %bitcast_dynamic-update-slice_fusion.q_ref, ...), custom_call_target="tpu_custom_call", output_to_operand_aliasing={{0}: (6, {}), {1}: (7, {}), {2}: (8, {})} | custom-call | flops 2147483648 | bytes 6000000 | tf_op jit(solution)/shard_map/attend_cross/pallas_call | solution.py:240
  139.7 1.0 collective-permute-done.14.refs_3_
  140.7 2.8 %collective-permute-done.8.refs_0_ = bf16[256,256]{1,0:T(8,128)(2,1)S(1)} collective-permute-done((bf16[256,256]{1,0:T(8,128)(2,1)S(1)}, bf16[256,256]{1,0:T(8,128)(2,1)S(1)}, u32[]{:S(2)}, u32[]{:S(2)}) %collective-permute-start.8) | collective-permute-done | bytes 131104 | tf_op jit(solution)/shard_map/ppermute | solution.py:290
  143.5 4.0 %attend_cross.5 = (bf16[64,1024]{1,0:T(8,128)(2,1)S(1)}, bf16[64,1024]{1,0:T(8,128)(2,1)S(1)}, bf16[64,1024]{1,0:T(8,128)(2,1)S(1)}, bf16[64,1024]{1,0:T(8,128)(2,1)S(1)}) custom-call(s32[1]{0:T(128)} %bitcast.19.upper_ref, bf16[8,64,1152]{2,1,0:T(8,128)(2,1)S(1)} %bitcast_dynamic-update-slice_fusion.q_ref, ...), custom_call_target="tpu_custom_call" | custom-call | flops 1073741824 | bytes 6000000 | tf_op jit(solution)/shard_map/attend_cross/pallas_call | solution.py:240
  147.5 1.2 collective-permute-start.23
  148.7 1.4 collective-permute-start.24
  150.1 1.6 collective-permute-start.25
  151.7 4.0 %attend_cross.4 = (bf16[64,1024]{1,0:T(8,128)(2,1)S(1)}, bf16[64,1024]{1,0:T(8,128)(2,1)S(1)}, bf16[64,1024]{1,0:T(8,128)(2,1)S(1)}, bf16[64,1024]{1,0:T(8,128)(2,1)S(1)}) custom-call(s32[1]{0:T(128)} %bitcast.19.upper_ref, bf16[8,64,1152]{2,1,0:T(8,128)(2,1)S(1)} %bitcast_dynamic-update-slice_fusion.q_ref, ...), custom_call_target="tpu_custom_call" | custom-call | flops 1073741824 | bytes 6000000 | tf_op jit(solution)/shard_map/attend_cross/pallas_call | solution.py:240
  155.7 3.3 %collective-permute-start.22 = (bf16[64,1024]{1,0:T(8,128)(2,1)S(1)}, bf16[64,1024]{1,0:T(8,128)(2,1)S(1)}, u32[]{:S(2)}, u32[]{:S(2)}) collective-permute-start(bf16[64,1024]{1,0:T(8,128)(2,1)S(1)} %get-tuple-element.61), channel_id=1, source_target_pairs={{0,7},{1,0},{2,1},{3,2},{4,3},{5,4},{6,5},{7,6},{8,15},{9,8},{10,9... | collective-permute-start | bytes 393224 | tf_op jit(solution)/shard_map/ppermute | solution.py:287
  159.0 0.4 collective-permute-start.27
  159.4 0.1 copy.13.used_ref
  159.5 0.2 collective-permute-done.26.refs_5_
  159.7 1.8 %collective-permute-done.22.refs_1_ = bf16[64,1024]{1,0:T(8,128)(2,1)S(1)} collective-permute-done((bf16[64,1024]{1,0:T(8,128)(2,1)S(1)}, bf16[64,1024]{1,0:T(8,128)(2,1)S(1)}, u32[]{:S(2)}, u32[]{:S(2)}) %collective-permute-start.22) | collective-permute-done | bytes 131104 | tf_op jit(solution)/shard_map/ppermute | solution.py:287
  161.6 4.9 %collective-permute-done.27.refs_6_ = bf16[64,1024]{1,0:T(8,128)(2,1)S(1)} collective-permute-done((bf16[64,1024]{1,0:T(8,128)(2,1)S(1)}, bf16[64,1024]{1,0:T(8,128)(2,1)S(1)}, u32[]{:S(2)}, u32[]{:S(2)}) %collective-permute-start.27) | collective-permute-done | bytes 131104 | tf_op jit(solution)/shard_map/ppermute | solution.py:287
  166.4 1.1 place_heads.1
  (45 shorter events, 0.5 us)
Async XLA Ops:
  0.6 16.0 %copy-start = (s32[16,144]{1,0:T(8,128)S(1)}, s32[16,144]{1,0:T(8,128)}, u32[]{:S(2)}) copy-start(s32[16,144]{1,0:T(8,128)} %param.7) | copy-start | bytes 27652
  1.4 1.2 copy-start.1
  2.7 16.8 %collective-permute-start = (bf16[64,1152]{1,0:T(8,128)(2,1)S(1)}, bf16[64,1152]{1,0:T(8,128)(2,1)}, u32[]{:S(2)}, u32[]{:S(2)}) collective-permute-start(bf16[64,1152]{1,0:T(8,128)(2,1)S(1)} %get-tuple-element.36), channel_id=1, source_target_pairs={{0,1},{1,2},{2,3},{3,4},{4,5},{5,6},{6,7},{7,0},{8,9},{9,10},{10,1... | collective-permute-start | bytes 442376 | tf_op jit(solution)/shard_map/ppermute | solution.py:287
  2.7 19.2 %collective-permute-start.1 = (bf16[64,1152]{1,0:T(8,128)(2,1)S(1)}, bf16[64,1152]{1,0:T(8,128)(2,1)}, u32[]{:S(2)}, u32[]{:S(2)}) collective-permute-start(bf16[64,1152]{1,0:T(8,128)(2,1)S(1)} %get-tuple-element.37), channel_id=1, source_target_pairs={{0,2},{1,3},{2,4},{3,5},{4,6},{5,7},{6,0},{7,1},{8,10},{9,11},{10,... | collective-permute-start | bytes 442376 | tf_op jit(solution)/shard_map/ppermute | solution.py:287
  4.3 18.6 %collective-permute-start.2 = (bf16[64,1152]{1,0:T(8,128)(2,1)S(1)}, bf16[64,1152]{1,0:T(8,128)(2,1)}, u32[]{:S(2)}, u32[]{:S(2)}) collective-permute-start(bf16[64,1152]{1,0:T(8,128)(2,1)S(1)} %get-tuple-element.38), channel_id=1, source_target_pairs={{0,3},{1,4},{2,5},{3,6},{4,7},{5,0},{6,1},{7,2},{8,11},{9,12},{10,... | collective-permute-start | bytes 442376 | tf_op jit(solution)/shard_map/ppermute | solution.py:287
  6.3 17.5 %collective-permute-start.3 = (bf16[64,1152]{1,0:T(8,128)(2,1)S(1)}, bf16[64,1152]{1,0:T(8,128)(2,1)S(1)}, u32[]{:S(2)}, u32[]{:S(2)}) collective-permute-start(bf16[64,1152]{1,0:T(8,128)(2,1)S(1)} %get-tuple-element.39), channel_id=1, source_target_pairs={{0,4},{1,5},{2,6},{3,7},{4,0},{5,1},{6,2},{7,3},{8,12},{9,13},{10,... | collective-permute-start | bytes 442376 | tf_op jit(solution)/shard_map/ppermute | solution.py:287
  8.4 9.8 %copy-start.3 = (s32[1,64]{1,0:T(1,128)S(1)}, s32[1,64]{1,0:T(1,128)}, u32[]{:S(2)}) copy-start(s32[1,64]{1,0:T(1,128)} %param.11) | copy-start | bytes 772
  8.4 15.5 %collective-permute-start.4 = (bf16[64,1152]{1,0:T(8,128)(2,1)S(1)}, bf16[64,1152]{1,0:T(8,128)(2,1)S(1)}, u32[]{:S(2)}, u32[]{:S(2)}) collective-permute-start(bf16[64,1152]{1,0:T(8,128)(2,1)S(1)} %get-tuple-element.40), channel_id=1, source_target_pairs={{0,5},{1,6},{2,7},{3,0},{4,1},{5,2},{6,3},{7,4},{8,13},{9,14},{10,... | collective-permute-start | bytes 442376 | tf_op jit(solution)/shard_map/ppermute | solution.py:287
  10.0 65.4 %all-to-all-start = ((bf16[16,40,2048]{2,1,0:T(8,128)(2,1)}), bf16[16,40,2048]{2,1,0:T(8,128)(2,1)}, u32[]{:S(2)}, u32[]{:S(2)}) async-start(bf16[16,40,2048]{2,1,0:T(8,128)(2,1)} %param.6), calls=%async_computation | async-start | bytes 5242880 | tf_op jit(solution)/shard_map/all_to_all | solution.py:292
  19.5 56.0 %copy-start.2 = (bf16[1,64,2048]{2,1,0:T(8,128)(2,1)S(1)}, bf16[1,64,2048]{2,1,0:T(8,128)(2,1)}, u32[]{:S(2)}) copy-start(bf16[1,64,2048]{2,1,0:T(8,128)(2,1)} %param.10) | copy-start | bytes 786436
  19.5 5.2 %collective-permute-start.5 = (bf16[64,1152]{1,0:T(8,128)(2,1)S(1)}, bf16[64,1152]{1,0:T(8,128)(2,1)S(1)}, u32[]{:S(2)}, u32[]{:S(2)}) collective-permute-start(bf16[64,1152]{1,0:T(8,128)(2,1)S(1)} %get-tuple-element.41), channel_id=1, source_target_pairs={{0,6},{1,7},{2,0},{3,1},{4,2},{5,3},{6,4},{7,5},{8,14},{9,15},{10,... | collective-permute-start | bytes 442376 | tf_op jit(solution)/shard_map/ppermute | solution.py:287
  21.9 3.3 %collective-permute-start.6 = (bf16[64,1152]{1,0:T(8,128)(2,1)S(1)}, bf16[64,1152]{1,0:T(8,128)(2,1)S(1)}, u32[]{:S(2)}, u32[]{:S(2)}) collective-permute-start(bf16[64,1152]{1,0:T(8,128)(2,1)S(1)} %get-tuple-element.42), channel_id=1, source_target_pairs={{0,7},{1,0},{2,1},{3,2},{4,3},{5,4},{6,5},{7,6},{8,15},{9,8},{10,9... | collective-permute-start | bytes 442376 | tf_op jit(solution)/shard_map/ppermute | solution.py:287
  79.8 5.4 %collective-permute-start.11 = (bf16[256,256]{1,0:T(8,128)(2,1)S(1)}, bf16[256,256]{1,0:T(8,128)(2,1)S(1)}, u32[]{:S(2)}, u32[]{:S(2)}) collective-permute-start(bf16[256,256]{1,0:T(8,128)(2,1)S(1)} %get-tuple-element.48), channel_id=1, source_target_pairs={{0,5},{1,6},{2,7},{3,0},{4,1},{5,2},{6,3},{7,4},{8,13},{9,14},{10,... | collective-permute-start | bytes 393224 | tf_op jit(solution)/shard_map/ppermute | solution.py:287
  80.7 7.9 %collective-permute-start.13 = (bf16[256,256]{1,0:T(8,128)(2,1)S(1)}, bf16[256,256]{1,0:T(8,128)(2,1)S(1)}, u32[]{:S(2)}, u32[]{:S(2)}) collective-permute-start(bf16[256,256]{1,0:T(8,128)(2,1)S(1)} %get-tuple-element.49), channel_id=1, source_target_pairs={{0,4},{1,5},{2,6},{3,7},{4,0},{5,1},{6,2},{7,3},{8,12},{9,13},{10,... | collective-permute-start | bytes 393224 | tf_op jit(solution)/shard_map/ppermute | solution.py:287
  82.1 7.2 %collective-permute-start.16 = (bf16[256,256]{1,0:T(8,128)(2,1)S(1)}, bf16[256,256]{1,0:T(8,128)(2,1)S(1)}, u32[]{:S(2)}, u32[]{:S(2)}) collective-permute-start(bf16[256,256]{1,0:T(8,128)(2,1)S(1)} %get-tuple-element.51), channel_id=1, source_target_pairs={{0,1},{1,2},{2,3},{3,4},{4,5},{5,6},{6,7},{7,0},{8,9},{9,10},{10,1... | collective-permute-start | bytes 393224 | tf_op jit(solution)/shard_map/ppermute | solution.py:287
  82.6 7.9 %collective-permute-start.18 = (bf16[256,256]{1,0:T(8,128)(2,1)S(1)}, bf16[256,256]{1,0:T(8,128)(2,1)S(1)}, u32[]{:S(2)}, u32[]{:S(2)}) collective-permute-start(bf16[256,256]{1,0:T(8,128)(2,1)S(1)} %get-tuple-element.52), channel_id=1, source_target_pairs={{0,7},{1,0},{2,1},{3,2},{4,3},{5,4},{6,5},{7,6},{8,15},{9,8},{10,9... | collective-permute-start | bytes 393224 | tf_op jit(solution)/shard_map/ppermute | solution.py:287
  85.0 7.0 %collective-permute-start.20 = (bf16[256,256]{1,0:T(8,128)(2,1)S(1)}, bf16[256,256]{1,0:T(8,128)(2,1)S(1)}, u32[]{:S(2)}, u32[]{:S(2)}) collective-permute-start(bf16[256,256]{1,0:T(8,128)(2,1)S(1)} %get-tuple-element.53), channel_id=1, source_target_pairs={{0,2},{1,3},{2,4},{3,5},{4,6},{5,7},{6,0},{7,1},{8,10},{9,11},{10,... | collective-permute-start | bytes 393224 | tf_op jit(solution)/shard_map/ppermute | solution.py:287
  85.2 8.1 %collective-permute-start.7 = (bf16[256,256]{1,0:T(8,128)(2,1)S(1)}, bf16[256,256]{1,0:T(8,128)(2,1)S(1)}, u32[]{:S(2)}, u32[]{:S(2)}) collective-permute-start(bf16[256,256]{1,0:T(8,128)(2,1)S(1)} %get-tuple-element.46), channel_id=1, source_target_pairs={{0,6},{1,7},{2,0},{3,1},{4,2},{5,3},{6,4},{7,5},{8,14},{9,15},{10,... | collective-permute-start | bytes 393224 | tf_op jit(solution)/shard_map/ppermute | solution.py:287
  88.6 7.2 %collective-permute-start.9 = (bf16[256,256]{1,0:T(8,128)(2,1)S(1)}, bf16[256,256]{1,0:T(8,128)(2,1)S(1)}, u32[]{:S(2)}, u32[]{:S(2)}) collective-permute-start(bf16[256,256]{1,0:T(8,128)(2,1)S(1)} %get-tuple-element.47), channel_id=1, source_target_pairs={{0,3},{1,4},{2,5},{3,6},{4,7},{5,0},{6,1},{7,2},{8,11},{9,12},{10,... | collective-permute-start | bytes 393224 | tf_op jit(solution)/shard_map/ppermute | solution.py:287
  89.2 34.6 %collective-permute-start.15 = (bf16[256,256]{1,0:T(8,128)(2,1)S(1)}, bf16[256,256]{1,0:T(8,128)(2,1)S(1)}, u32[]{:S(2)}, u32[]{:S(2)}) collective-permute-start(bf16[256,256]{1,0:T(8,128)(2,1)S(1)} %get-tuple-element.50.refs_0_), channel_id=1, source_target_pairs={{0,8},{1,9},{2,10},{3,11},{4,12},{5,13},{6,14},{7,15},{16,24},{17,... | collective-permute-start | bytes 393224 | tf_op jit(solution)/shard_map/ppermute | solution.py:290
  90.5 36.1 %collective-permute-start.17 = (bf16[256,256]{1,0:T(8,128)(2,1)S(1)}, bf16[256,256]{1,0:T(8,128)(2,1)S(1)}, u32[]{:S(2)}, u32[]{:S(2)}) collective-permute-start(bf16[256,256]{1,0:T(8,128)(2,1)S(1)} %collective-permute-done.16.refs_1_), channel_id=1, source_target_pairs={{0,8},{1,9},{2,10},{3,11},{4,12},{5,13},{6,14},{7,15},{16,24},{17,... | collective-permute-start | bytes 393224 | tf_op jit(solution)/shard_map/ppermute | solution.py:290
  92.0 37.4 %collective-permute-start.19 = (bf16[256,256]{1,0:T(8,128)(2,1)S(1)}, bf16[256,256]{1,0:T(8,128)(2,1)S(1)}, u32[]{:S(2)}, u32[]{:S(2)}) collective-permute-start(bf16[256,256]{1,0:T(8,128)(2,1)S(1)} %collective-permute-done.18.refs_7_), channel_id=1, source_target_pairs={{0,8},{1,9},{2,10},{3,11},{4,12},{5,13},{6,14},{7,15},{16,24},{17,... | collective-permute-start | bytes 393224 | tf_op jit(solution)/shard_map/ppermute | solution.py:290
  93.3 38.9 %collective-permute-start.21 = (bf16[256,256]{1,0:T(8,128)(2,1)S(1)}, bf16[256,256]{1,0:T(8,128)(2,1)S(1)}, u32[]{:S(2)}, u32[]{:S(2)}) collective-permute-start(bf16[256,256]{1,0:T(8,128)(2,1)S(1)} %collective-permute-done.20.refs_2_), channel_id=1, source_target_pairs={{0,8},{1,9},{2,10},{3,11},{4,12},{5,13},{6,14},{7,15},{16,24},{17,... | collective-permute-start | bytes 393224 | tf_op jit(solution)/shard_map/ppermute | solution.py:290
  95.8 43.9 %collective-permute-start.10 = (bf16[256,256]{1,0:T(8,128)(2,1)S(1)}, bf16[256,256]{1,0:T(8,128)(2,1)S(1)}, u32[]{:S(2)}, u32[]{:S(2)}) collective-permute-start(bf16[256,256]{1,0:T(8,128)(2,1)S(1)} %collective-permute-done.9.refs_3_), channel_id=1, source_target_pairs={{0,8},{1,9},{2,10},{3,11},{4,12},{5,13},{6,14},{7,15},{16,24},{17,... | collective-permute-start | bytes 393224 | tf_op jit(solution)/shard_map/ppermute | solution.py:290
  123.8 15.9 %collective-permute-start.12 = (bf16[256,256]{1,0:T(8,128)(2,1)S(1)}, bf16[256,256]{1,0:T(8,128)(2,1)S(1)}, u32[]{:S(2)}, u32[]{:S(2)}) collective-permute-start(bf16[256,256]{1,0:T(8,128)(2,1)S(1)} %collective-permute-done.11.refs_5_), channel_id=1, source_target_pairs={{0,8},{1,9},{2,10},{3,11},{4,12},{5,13},{6,14},{7,15},{16,24},{17,... | collective-permute-start | bytes 393224 | tf_op jit(solution)/shard_map/ppermute | solution.py:290
  126.6 14.0 %collective-permute-start.14 = (bf16[256,256]{1,0:T(8,128)(2,1)S(1)}, bf16[256,256]{1,0:T(8,128)(2,1)S(1)}, u32[]{:S(2)}, u32[]{:S(2)}) collective-permute-start(bf16[256,256]{1,0:T(8,128)(2,1)S(1)} %collective-permute-done.13.refs_4_), channel_id=1, source_target_pairs={{0,8},{1,9},{2,10},{3,11},{4,12},{5,13},{6,14},{7,15},{16,24},{17,... | collective-permute-start | bytes 393224 | tf_op jit(solution)/shard_map/ppermute | solution.py:290
  129.4 14.0 %collective-permute-start.8 = (bf16[256,256]{1,0:T(8,128)(2,1)S(1)}, bf16[256,256]{1,0:T(8,128)(2,1)S(1)}, u32[]{:S(2)}, u32[]{:S(2)}) collective-permute-start(bf16[256,256]{1,0:T(8,128)(2,1)S(1)} %collective-permute-done.7.refs_6_), channel_id=1, source_target_pairs={{0,8},{1,9},{2,10},{3,11},{4,12},{5,13},{6,14},{7,15},{16,24},{17,... | collective-permute-start | bytes 393224 | tf_op jit(solution)/shard_map/ppermute | solution.py:290
  147.5 11.5 %collective-permute-start.23 = (bf16[64,1024]{1,0:T(8,128)(2,1)S(1)}, bf16[64,1024]{1,0:T(8,128)(2,1)S(1)}, u32[]{:S(2)}, u32[]{:S(2)}) collective-permute-start(bf16[64,1024]{1,0:T(8,128)(2,1)S(1)} %get-tuple-element.62), channel_id=1, source_target_pairs={{0,6},{1,7},{2,0},{3,1},{4,2},{5,3},{6,4},{7,5},{8,14},{9,15},{10,... | collective-permute-start | bytes 393224 | tf_op jit(solution)/shard_map/ppermute | solution.py:287
  148.7 10.7 %collective-permute-start.24 = (bf16[64,1024]{1,0:T(8,128)(2,1)S(1)}, bf16[64,1024]{1,0:T(8,128)(2,1)S(1)}, u32[]{:S(2)}, u32[]{:S(2)}) collective-permute-start(bf16[64,1024]{1,0:T(8,128)(2,1)S(1)} %get-tuple-element.63), channel_id=1, source_target_pairs={{0,5},{1,6},{2,7},{3,0},{4,1},{5,2},{6,3},{7,4},{8,13},{9,14},{10,... | collective-permute-start | bytes 393224 | tf_op jit(solution)/shard_map/ppermute | solution.py:287
  150.1 9.5 %collective-permute-start.25 = (bf16[64,1024]{1,0:T(8,128)(2,1)S(1)}, bf16[64,1024]{1,0:T(8,128)(2,1)S(1)}, u32[]{:S(2)}, u32[]{:S(2)}) collective-permute-start(bf16[64,1024]{1,0:T(8,128)(2,1)S(1)} %get-tuple-element.64), channel_id=1, source_target_pairs={{0,4},{1,5},{2,6},{3,7},{4,0},{5,1},{6,2},{7,3},{8,12},{9,13},{10,... | collective-permute-start | bytes 393224 | tf_op jit(solution)/shard_map/ppermute | solution.py:287
  151.7 8.1 %collective-permute-start.26 = (bf16[64,1024]{1,0:T(8,128)(2,1)S(1)}, bf16[64,1024]{1,0:T(8,128)(2,1)S(1)}, u32[]{:S(2)}, u32[]{:S(2)}) collective-permute-start(bf16[64,1024]{1,0:T(8,128)(2,1)S(1)} %get-tuple-element.65), channel_id=1, source_target_pairs={{0,3},{1,4},{2,5},{3,6},{4,7},{5,0},{6,1},{7,2},{8,11},{9,12},{10,... | collective-permute-start | bytes 393224 | tf_op jit(solution)/shard_map/ppermute | solution.py:287
  155.7 5.8 %collective-permute-start.22 = (bf16[64,1024]{1,0:T(8,128)(2,1)S(1)}, bf16[64,1024]{1,0:T(8,128)(2,1)S(1)}, u32[]{:S(2)}, u32[]{:S(2)}) collective-permute-start(bf16[64,1024]{1,0:T(8,128)(2,1)S(1)} %get-tuple-element.61), channel_id=1, source_target_pairs={{0,7},{1,0},{2,1},{3,2},{4,3},{5,4},{6,5},{7,6},{8,15},{9,8},{10,9... | collective-permute-start | bytes 393224 | tf_op jit(solution)/shard_map/ppermute | solution.py:287
  159.0 7.4 %collective-permute-start.27 = (bf16[64,1024]{1,0:T(8,128)(2,1)S(1)}, bf16[64,1024]{1,0:T(8,128)(2,1)S(1)}, u32[]{:S(2)}, u32[]{:S(2)}) collective-permute-start(bf16[64,1024]{1,0:T(8,128)(2,1)S(1)} %get-tuple-element.66), channel_id=1, source_target_pairs={{0,2},{1,3},{2,4},{3,5},{4,6},{5,7},{6,0},{7,1},{8,10},{9,11},{10,... | collective-permute-start | bytes 393224 | tf_op jit(solution)/shard_map/ppermute | solution.py:287
  159.4 7.0 %collective-permute-start.28 = (bf16[64,1024]{1,0:T(8,128)(2,1)S(1)}, bf16[64,1024]{1,0:T(8,128)(2,1)S(1)}, u32[]{:S(2)}, u32[]{:S(2)}) collective-permute-start(bf16[64,1024]{1,0:T(8,128)(2,1)S(1)} %get-tuple-element.67), channel_id=1, source_target_pairs={{0,1},{1,2},{2,3},{3,4},{4,5},{5,6},{6,7},{7,0},{8,9},{9,10},{10,1... | collective-permute-start | bytes 393224 | tf_op jit(solution)/shard_map/ppermute | solution.py:287
